TPU v7x, 32 devices: a whole 2x2x4 slice. The times are simulated.
32 devices in a mesh: cfg: 2 (over y), ta: 4 (over z), xyz: 4 (over x, core).
Axes of the slice: x: 2, y: 2, z: 4, core: 2. Of those that a mesh axis runs over, the one named last changes fastest.
Arguments:
- sink: float32 [24, 4, 3, 2, 4, 32, 128], P('cfg', None, None, None, 'ta', 'xyz'), parts along dimension 0, may hold values from -6 to 6
- links: float32 [16, 4, 3, 3, 2, 4, 32, 128], P('cfg', None, None, None, None, 'ta', 'xyz'), parts along dimension 0, may hold values from -2 to 2
- section_index: int32 [2, 3], replicated, may hold values from 0 to 7
- momenta: int32 [33, 3], replicated, may hold values from -3 to 3
- source: int32 [3], replicated, may hold values from 0 to 15
Outputs:
- adjoint: float32 [24, 4, 3, 2, 4, 32, 128], P('cfg', None, None, None, 'ta', 'xyz'), parts along dimension 0
- correlator: float32 [4, 33, 4], P('cfg', None, 'ta'), parts along dimension 0
There are 2 independent parts, one for each index of `cfg`. A program takes and returns all parts, laid end to end along the dimension named above; an argument that names none is the same for every part. Nothing has to cross between parts.
All inputs are finite; a program needn't handle non-finite values.
Results may differ from a plain program's by a relative error of at most 0.000068.
Values sent between devices are 32-bit elements; how exact they have to be, the bound alone decides.
A program may use at most 128 MiB of HBM per device.

v0:
```python
import functools
import math

import jax
import jax.numpy as jnp
from jax import lax
from jax.experimental import pallas as pl
from jax.experimental.pallas import tpu as pltpu
from jax.sharding import PartitionSpec as P

NMOM = 33
STEPS = 2
NY = 16
NZ = 8


flow_step = 0.05


def phase_table(xcoord, nx_total, momenta, source):
    plane_index = jnp.arange(NY * NZ, dtype=jnp.int32)
    ycoord = plane_index // NZ
    zcoord = plane_index % NZ
    dist_x = jnp.mod(xcoord - source[0], nx_total)
    dist_y = jnp.mod(ycoord - source[1], NY)
    dist_z = jnp.mod(zcoord - source[2], NZ)
    frac_x = jnp.mod(momenta[:, 0:1] * dist_x[None, :], nx_total).astype(jnp.float32) / float(
        nx_total
    )
    frac_y = jnp.mod(momenta[:, 1:2] * dist_y[None, :], NY).astype(jnp.float32) / float(NY)
    frac_z = jnp.mod(momenta[:, 2:3] * dist_z[None, :], NZ).astype(jnp.float32) / float(NZ)
    frac = frac_x[:, :, None] + frac_y[:, None, :] + frac_z[:, None, :]
    angle = 2.0 * math.pi * frac
    table = jnp.concatenate([jnp.cos(angle), -jnp.sin(angle)], axis=0)
    return table.reshape(2 * NMOM, xcoord.shape[0] * NY * NZ)


MESH = pl.DeviceIdType.MESH
SECTIONS = 3 * STEPS
BLOCK = 75


def remote(src, dst, send_sem, recv_sem, axis, peer):
    return pltpu.make_async_remote_copy(
        src_ref=src, dst_ref=dst, send_sem=send_sem, recv_sem=recv_sem,
        device_id={axis: peer}, device_id_type=MESH,
    )


def multiply(link, vec, conj):
    real = imag = None
    for k in range(3):
        if conj:
            lr, li = link[k, :, 0], link[k, :, 1]
        else:
            lr, li = link[:, k, 0], link[:, k, 1]
        vr, vi = vec[k, 0][None], vec[k, 1][None]
        if conj:
            r, i = lr * vr + li * vi, lr * vi - li * vr
        else:
            r, i = lr * vr - li * vi, lr * vi + li * vr
        real = r if real is None else real + r
        imag = i if imag is None else imag + i
    return real, imag


def roll3(x, amount, axis):
    shape = x.shape
    flat = x.reshape((-1,) + shape[-2:])
    return pltpu.roll(flat, amount % flat.shape[axis], axis).reshape(shape)


def kernel(n, nx, nc, lo, hi, parts, sink_ref, link_ref, table_ref, out_ref, proj_ref,
           lam, later, mixed, lk, back, hs, hr, pj,
           loc_sem, fs_sem, fr_sem, us_sem, ur_sem, ds_sem, dr_sem,
           hss_sem, hsr_sem, os_sem, or_sem, ps_sem, pr_sem):
    me = lax.axis_index("ta")
    mx = lax.axis_index("xyz")
    worker = jnp.logical_and(me >= lo, me < hi)
    mine = me - lo
    share = nc // parts
    left, right = lax.rem(mx + nx - 1, nx), lax.rem(mx + 1, nx)
    sub = lax.broadcasted_iota(jnp.int32, (8, 128), 0)
    zc = lax.broadcasted_iota(jnp.int32, (8, 128), 1) % NZ

    barrier = pltpu.get_barrier_semaphore()
    for d in range(1, n):
        pl.semaphore_signal(barrier, inc=1, device_id={"ta": lax.rem(me + d, n)}, device_id_type=MESH)
    for d in range(1, nx):
        pl.semaphore_signal(barrier, inc=1, device_id={"xyz": lax.rem(mx + d, nx)}, device_id_type=MESH)

    def own_copy():
        return pltpu.make_async_copy(sink_ref.at[pl.ds(mine * nc, nc)], lam.at[me], loc_sem.at[SECTIONS])

    @pl.when(worker)
    def _():
        own_copy().start()

    for s in range(SECTIONS):
        pltpu.make_async_copy(link_ref.at[s], lk.at[s, me], loc_sem.at[s]).start()
    pl.semaphore_wait(barrier, n + nx - 2)

    def field_copy(j, source):
        return remote(sink_ref.at[pl.ds(j * nc, nc)], lam.at[source],
                      fs_sem.at[j], fr_sem.at[source], "ta", lo + j)

    for j in range(hi - lo):
        @pl.when(me != lo + j)
        def _():
            field_copy(j, me).start()

    def up_copy(s, h):
        blk = lax.rem(me - h + n, n)
        return remote(lk.at[s, blk], lk.at[s, blk], us_sem.at[s, h], ur_sem.at[s, h],
                      "ta", lax.rem(me + 1, n))

    def down_copy(s, h):
        blk = lax.rem(me + h, n)
        return remote(lk.at[s, blk], lk.at[s, blk], ds_sem.at[s, h], dr_sem.at[s, h],
                      "ta", lax.rem(me + n - 1, n))

    def has_up(h):
        return jnp.logical_and(me - h >= 0, me + 1 <= hi - 1)

    def has_down(h):
        return jnp.logical_and(me + h <= n - 1, me - 1 >= lo)

    def start_hop(s, h):
        @pl.when(has_up(h))
        def _():
            up_copy(s, h).start()

        @pl.when(has_down(h))
        def _():
            down_copy(s, h).start()

    def wait_hop(s, h):
        @pl.when(jnp.logical_and(me - 1 - h >= 0, me <= hi - 1))
        def _():
            up_copy(s, h).wait_recv()

        @pl.when(jnp.logical_and(me + 1 + h <= n - 1, me >= lo))
        def _():
            down_copy(s, h).wait_recv()

    for s in range(SECTIONS):
        pltpu.make_async_copy(link_ref.at[s], lk.at[s, me], loc_sem.at[s]).wait()
        if s < 2:
            start_hop(s, 0)
    @pl.when(worker)
    def _():
        own_copy().wait()
        for d in range(1, n):
            field_copy(0, lax.rem(me + d, n)).wait_recv()

    def halo_copy(s, side, part):
        peer = (left, right)[side]
        return remote(hs.at[s % 2, side, part], hr.at[s % 2, side, part], hss_sem.at[s, side, part],
                      hsr_sem.at[s, side, part], "xyz", peer)

    def put_halo(s, t, q, value):
        hs[s % 2, 0, q // share, t, q % share, 0:6] = value[:, 0, :]
        hs[s % 2, 1, q // share, t, q % share, 0:6] = value[:, 7, :]

    def first_halo(j, carry):
        t, q = j // nc, j % nc
        put_halo(0, t, q, lam[t, q])
        return carry

    @pl.when(worker)
    def _():
        lax.fori_loop(0, n * nc, first_halo, 0)
        for part in range(parts):
            for side in range(2):
                halo_copy(0, side, part).start()

    def prepare(s):
        def at_time(t, carry):
            ux = roll3(lk[s, t, 18:36], 1, 1)
            for j in range(18):
                row = lk[s, t, 72 + j // 8, j % 8:j % 8 + 1, :]
                back[t, 0, j] = jnp.where(sub == 0, jnp.broadcast_to(row, (8, 128)), ux[j])
            back[t, 1] = roll3(lk[s, t, 36:54], NZ, 2)
            uz = lk[s, t, 54:72]
            back[t, 2] = jnp.where((zc == 0)[None], roll3(uz, 1 - NZ, 2), roll3(uz, 1, 2))
            return carry

        lax.fori_loop(0, n, at_time, 0)

    def lap(s, part, source, epilogue):
        par = s % 2

        def at_time(t, carry):
            prev, following = lax.rem(t + n - 1, n), lax.rem(t + 1, n)

            def links(ref_block):
                return ref_block.reshape(3, 3, 2, 8, 128)

            def at_spinor(w, inner):
                q = part * share + w
                v = source[t, q]

                def add(acc, r, i):
                    return (r, i) if acc is None else (acc[0] + r, acc[1] + i)

                def vec(x):
                    return x.reshape(3, 2, 8, 128)

                acc = None
                r, i = multiply(links(lk[s, t, 0:18]), vec(source[following, q]), False)
                acc = add(acc, r, i)
                r, i = multiply(links(lk[s, prev, 0:18]), vec(source[prev, q]), True)
                acc = add(acc, r, i)
                high = jnp.broadcast_to(hr[par, 0, part, t, w, 0:6][:, None, :], (6, 8, 128))
                low = jnp.broadcast_to(hr[par, 1, part, t, w, 0:6][:, None, :], (6, 8, 128))
                vf = jnp.where((sub == 7)[None], high, roll3(v, -1, 1))
                r, i = multiply(links(lk[s, t, 18:36]), vec(vf), False)
                acc = add(acc, r, i)
                vb = jnp.where((sub == 0)[None], low, roll3(v, 1, 1))
                r, i = multiply(links(back[t, 0]), vec(vb), True)
                acc = add(acc, r, i)
                r, i = multiply(links(lk[s, t, 36:54]), vec(roll3(v, -NZ, 2)), False)
                acc = add(acc, r, i)
                r, i = multiply(links(back[t, 1]), vec(roll3(v, NZ, 2)), True)
                acc = add(acc, r, i)
                vf = jnp.where((zc == NZ - 1)[None], roll3(v, NZ - 1, 2), roll3(v, -1, 2))
                r, i = multiply(links(lk[s, t, 54:72]), vec(vf), False)
                acc = add(acc, r, i)
                vb = jnp.where((zc == 0)[None], roll3(v, 1 - NZ, 2), roll3(v, 1, 2))
                r, i = multiply(links(back[t, 2]), vec(vb), True)
                acc = add(acc, r, i)
                hop = jnp.stack([acc[0], acc[1]], axis=1).reshape(6, 8, 128)
                nxt = epilogue(t, q, hop - 8.0 * v, v)
                put_halo(s + 1, t, q, nxt)
                return inner

            lax.fori_loop(0, share, at_spinor, 0)
            return carry

        lax.fori_loop(0, n, at_time, 0)

    def ep_later(t, q, value, v):
        value = (0.75 * flow_step) * value
        later[t, q] = value
        return value

    def ep_middle(t, q, value, v):
        middle = lam[t, q] + (8.0 * flow_step / 9.0) * value
        lam[t, q] = middle + v
        value = (0.25 * flow_step) * middle - (2.0 * flow_step / 9.0) * v
        mixed[t, q] = value
        return value

    def ep_last(t, q, value, v):
        value = lam[t, q] + value
        lam[t, q] = value
        return value

    def out_copy(t, part, j):
        return remote(lam.at[t, pl.ds(part * share, share)],
                      out_ref.at[pl.ds(j * nc + part * share, share)],
                      os_sem.at[t, part], or_sem.at[j, part], "ta", t)

    hops = hi - 1

    def pass_on(s):
        for h in range(hops - 1):
            wait_hop(s, h)
            start_hop(s, h + 1)

    pass_on(0)

    def step_body(i, carry):
        for k, (source, epilogue) in enumerate(((lam, ep_later), (later, ep_middle), (mixed, ep_last))):
            s = i * 3 + k
            @pl.when(s + 1 < SECTIONS)
            def _():
                pass_on(s + 1)

            @pl.when(s + 2 < SECTIONS)
            def _():
                start_hop(s + 2, 0)

            wait_hop(s, hops - 1)

            @pl.when(worker)
            def _():
                prepare(s)

                def at_part(part, inner):
                    for side in range(2):
                        halo_copy(s, side, part).wait()
                    lap(s, part, source, epilogue)

                    @pl.when(s + 1 < SECTIONS)
                    def _():
                        for side in range(2):
                            halo_copy(s + 1, side, part).start()

                    @pl.when(s + 1 == SECTIONS)
                    def _():
                        for d in range(1, n):
                            out_copy(lax.rem(me + d, n), part, mine).start()
                    return inner

                lax.fori_loop(0, parts, at_part, 0)
        return carry

    lax.fori_loop(0, STEPS, step_body, 0)

    @pl.when(worker)
    def _():
        out_ref[pl.ds(mine * nc, nc)] = lam[me]

    for j in range(hi - lo):
        @pl.when(me != lo + j)
        def _():
            field_copy(j, me).wait_send()

    def drain(s, carry):
        for h in range(hops):
            @pl.when(has_up(h))
            def _():
                up_copy(s, h).wait_send()

            @pl.when(has_down(h))
            def _():
                down_copy(s, h).wait_send()
        return carry

    lax.fori_loop(0, SECTIONS, drain, 0)
    @pl.when(worker)
    def _():
        for part in range(parts):
            for d in range(1, n):
                out_copy(lax.rem(me + d, n), part, mine).wait_send()

    for j in range(hi - lo):
        @pl.when(me != lo + j)
        def _():
            for part in range(parts):
                out_copy(lo + j, part, j).wait_recv()

    def squares(j, acc):
        block = out_ref[pl.ds(j * 4, 4)]
        sq = jnp.sum(block * block, axis=1)
        return acc + ((sq[0] + sq[1]) - (sq[2] + sq[3]))

    density = lax.fori_loop(0, sink_ref.shape[0] // 4, squares, jnp.zeros((8, 128), jnp.float32))
    pj[mx] = jnp.sum(table_ref[...] * density[None], axis=1)

    def proj_copy(d):
        return remote(pj.at[mx], pj.at[mx], ps_sem.at[d - 1], pr_sem.at[d - 1],
                      "xyz", lax.rem(mx + d, nx))

    for d in range(1, nx):
        proj_copy(d).start()
    for d in range(1, nx):
        proj_copy(d).wait()
    total = pj[0]
    for j in range(1, nx):
        total = total + pj[j]
    proj_ref[...] = jnp.broadcast_to(jnp.sum(total, axis=1, keepdims=True), total.shape)


def body(n, nx, sink, links, section_index, momenta, source):
    space_cells = sink.shape[5]
    spinors = sink.shape[0] * sink.shape[1]
    lo = n // 4 if spinors % (n - 2 * (n // 4)) == 0 else 0
    hi = n - lo
    nc = spinors // (hi - lo)
    parts = 3 if nc % 3 == 0 else 1
    order = jnp.concatenate([section_index[step, ::-1] for step in reversed(range(STEPS))])
    chosen = jnp.take(links, order, axis=0).reshape(SECTIONS, 72, space_cells, NY * NZ)
    rows = chosen[:, 18:36, space_cells - 1, :]
    rows = lax.ppermute(rows, "xyz", [(i, (i + 1) % nx) for i in range(nx)])
    rows = jnp.pad(rows, ((0, 0), (0, 6), (0, 0))).reshape(SECTIONS, 3, 8, NY * NZ)
    blocks = jnp.concatenate([chosen, rows], axis=1)
    nx_total = space_cells * nx
    xcoord = lax.axis_index("xyz") * space_cells + jnp.arange(space_cells, dtype=jnp.int32)
    table = phase_table(xcoord, nx_total, momenta, source)
    table = table.reshape(2 * NMOM, space_cells, NY * NZ)
    tile = (space_cells, NY * NZ)
    field = pltpu.VMEM((n, nc, 6) + tile, jnp.float32)
    dma = pltpu.SemaphoreType.DMA
    out, proj = pl.pallas_call(
        functools.partial(kernel, n, nx, nc, lo, hi, parts),
        out_shape=(
            jax.ShapeDtypeStruct((spinors, 6) + tile, jnp.float32),
            jax.ShapeDtypeStruct((2 * NMOM, NY * NZ), jnp.float32),
        ),
        in_specs=[
            pl.BlockSpec(memory_space=pl.ANY),
            pl.BlockSpec(memory_space=pl.ANY),
            pl.BlockSpec(memory_space=pltpu.VMEM),
        ],
        out_specs=(pl.BlockSpec(memory_space=pltpu.VMEM), pl.BlockSpec(memory_space=pltpu.VMEM)),
        scratch_shapes=[
            field, field, field,
            pltpu.VMEM((SECTIONS, n, BLOCK) + tile, jnp.float32),
            pltpu.VMEM((n, 3, 18) + tile, jnp.float32),
            pltpu.VMEM((2, 2, parts, n, nc // parts, 8, NY * NZ), jnp.float32),
            pltpu.VMEM((2, 2, parts, n, nc // parts, 8, NY * NZ), jnp.float32),
            pltpu.VMEM((nx, 2 * NMOM, NY * NZ), jnp.float32),
            dma((SECTIONS + 1,)),
            dma((hi - lo,)), dma((n,)),
            dma((SECTIONS, n - 1)), dma((SECTIONS, n - 1)),
            dma((SECTIONS, n - 1)), dma((SECTIONS, n - 1)),
            dma((SECTIONS, 2, parts)), dma((SECTIONS, 2, parts)),
            dma((n, parts)), dma((hi - lo, parts)),
            dma((nx - 1,)), dma((nx - 1,)),
        ],
        compiler_params=pltpu.CompilerParams(
            collective_id=0, has_side_effects=True, vmem_limit_bytes=60 * 1024 * 1024
        ),
    )(sink.reshape((spinors, 6) + tile), blocks, table)
    scale = 1.0 / math.sqrt(576.0 * nx_total * NY * NZ)
    correlator = (proj[:, :1] * scale).reshape(2, NMOM, 1)
    return (out.reshape(sink.shape), correlator)


def solution(mesh):
    in_specs = (
        P("cfg", None, None, None, "ta", "xyz", None),
        P("cfg", None, None, None, None, "ta", "xyz", None),
        P(),
        P(),
        P(),
    )
    out_specs = (P("cfg", None, None, None, "ta", "xyz", None), P("cfg", None, "ta"))
    step = functools.partial(body, mesh.shape["ta"], mesh.shape["xyz"])
    return jax.shard_map(step, mesh=mesh, in_specs=in_specs, out_specs=out_specs, check_vma=False)
```

profile of v0, /device:TPU:0, one launch (start us, length us, event | category | flops | bytes accessed | tf_op | source)
XLA Modules:
  0.0 177.7 jit_solution(9229025121455817402)
XLA Ops:
  0.6 0.0 copy-start
  0.6 0.8 fusion.16
  1.5 0.1 rev.7
  1.6 0.1 rev.6
  1.7 0.1 fusion.15
  1.8 0.6 copy-done
  2.3 1.9 %gather_fusion = f32[6,4,3,3,2,8,128]{6,5,4,3,2,1,0:T(8,128)} fusion(f32[8,4,3,3,2,8,128]{6,5,4,3,2,1,0:T(8,128)S(1)} %bitcast.27, s32[1024]{0:T(1024)S(1)} %pad_clamp_fusion), kind=kCustom, calls=%fused_computation | custom fusion | bytes 3538968 | tf_op jit(solution)/shard_map/jit(_take)/gather | solution.py:374
  4.2 0.1 compare_and_fusion
  4.3 0.0 copy-start.2
  4.3 0.0 copy-start.3
  4.3 1.7 broadcast_select_fusion
  6.0 0.0 copy-start.1
  6.0 1.2 copy-done.1
  7.3 0.5 collective-permute-start
  7.8 0.0 copy-done.2
  7.9 0.7 fusion.17
  8.5 0.7 and_select_fusion.2
  9.2 0.0 copy-done.3
  9.2 0.7 and_select_fusion
  9.9 0.7 and_select_fusion.4
  10.6 0.1 fusion.2
  10.6 0.1 fusion.4
  10.7 0.6 fusion
  11.3 0.7 pad_maximum_fusion.1.table_ref
  12.0 0.0 collective-permute-done
  12.0 2.8 %pad_maximum_fusion.link_ref = f32[6,75,8,128]{3,2,1,0:T(8,128)} fusion(f32[6,3,8,128]{3,2,1,0:T(8,128)S(1)} %pad_bitcast_fusion, f32[6,72,8,128]{3,2,1,0:T(8,128)} %copy-done.1), kind=kLoop, calls=%fused_computation.1 | loop fusion | flops 460800 | bytes 3686400 | tf_op jit(solution)/shard_map/concatenate | solution.py:378
  14.9 158.9 %shard_map.68 = (f32[48,6,8,128]{3,2,1,0:T(8,128)}, f32[66,128]{1,0:T(8,128)}) custom-call(f32[48,6,8,128]{3,2,1,0:T(8,128)} %bitcast.29, f32[6,75,8,128]{3,2,1,0:T(8,128)} %pad_maximum_fusion.link_ref, f32[66,8,128]{2,1,0:T(8,128)} %pad_maximum_fusion.1.table_ref), custom_call_target="tpu_custom_call" | custom-call | tf_op jit(solution)/shard_map/pallas_call | solution.py:386
  173.8 0.9 multiply_reduce_fusion
  174.7 0.7 reshape.298
  175.4 2.4 %copy.15 = f32[12,4,3,2,1,8,128]{6,5,4,3,2,1,0:T(8,128)} copy(f32[12,4,3,2,1,8,128]{6,5,4,3,2,1,0:T(8,128)} %bitcast.30) | data formatting | bytes 2359296
  (5 shorter events, 0.1 us)
Async XLA Ops:
  0.6 1.7 copy-start
  4.3 3.5 %copy-start.2 = (s32[3]{0:T(128)S(1)}, s32[3]{0:T(128)}, u32[]{:S(2)}) copy-start(s32[3]{0:T(128)} %param.9) | copy-start | bytes 40
  4.3 4.9 %copy-start.3 = (s32[33,3]{0,1:T(4,128)S(1)}, s32[33,3]{0,1:T(4,128)}, u32[]{:S(2)}) copy-start(s32[33,3]{0,1:T(4,128)} %param.8) | copy-start | bytes 1192
  6.0 1.2 copy-start.1
  7.3 4.7 %collective-permute-start = (f32[6,18,128]{2,1,0:T(8,128)S(1)}, f32[6,18,128]{2,1,0:T(8,128)S(1)}, u32[]{:S(2)}, u32[]{:S(2)}) collective-permute-start(f32[6,18,128]{2,1,0:T(8,128)S(1)} %bitcast.31), channel_id=1, source_target_pairs={{0,1},{1,2},{2,3},{3,0},{4,5},{5,6},{6,7},{7,4},{8,9},{9,10},{10,1... | collective-permute-start | bytes 165896 | tf_op jit(solution)/shard_map/ppermute | solution.py:376
where the time goes:
time: 178 us
  Pallas kernels  159 us (89%)
  other arithmetic  9.04 us (5%)
  local copies, waits for them, and re-layouts  8.47 us (5%)
    pallas_call x1, Pallas kernels, body(): pl.pallas_call(functools.partial(kernel, n, nx, nc, lo, hi, parts), out_s...  159 us
    unnamed x10, local copies, waits for them, and re-layouts  4.17 us
  transfers between devices with their start and end apart: 1, of which 0 were waited for; matrix products, arithmetic and copies ran while one was open for 2% of the time, Pallas kernels for 0%

commit v1 on v0

v1 whole, which is shorter than its diff:
```python
import functools
import math

import jax
import jax.numpy as jnp
from jax import lax
from jax.experimental import pallas as pl
from jax.experimental.pallas import tpu as pltpu
from jax.sharding import PartitionSpec as P

STEPS = 2
NY = 16
NZ = 8
SECTIONS = 3 * STEPS
MESH = pl.DeviceIdType.MESH

flow_step = 0.05


def remote(src, dst, send_sem, recv_sem, axis, peer):
    return pltpu.make_async_remote_copy(
        src_ref=src, dst_ref=dst, send_sem=send_sem, recv_sem=recv_sem,
        device_id={axis: peer}, device_id_type=MESH,
    )


def roll3(x, amount, axis):
    shape = x.shape
    flat = x.reshape((-1,) + shape[-2:])
    return pltpu.roll(flat, amount % flat.shape[axis], axis).reshape(shape)


def hop(acc, link, x, conj):
    one, two, three = acc
    for k in range(3):
        vr, vi = x[2 * k], x[2 * k + 1]
        vs = (vr + vi)[None]
        if conj:
            block = link[k]
            a, b, c = block[:, 0] * vs, block[:, 2] * vi[None], block[:, 1] * vr[None]
            two = -b if two is None else two - b
            three = -c if three is None else three - c
        else:
            block = link[:, k]
            a, b, c = block[:, 0] * vs, block[:, 1] * vi[None], block[:, 2] * vr[None]
            two = b if two is None else two + b
            three = c if three is None else three + c
        one = a if one is None else one + a
    return one, two, three


def kernel(n, nx, nc, lo, hi, parts, nmom, order_ref, source_ref, momenta_ref, sink_ref, link_ref,
           out_ref, proj_ref,
           raw, lk, cur, lam, later, mixed, hs, hr, rs, rr, table, dens, pjs, pjr, pjt, pjf,
           raw_sem, loc_sem, fs_sem, fr_sem, ls_sem, lr_sem,
           hss_sem, hsr_sem, rs_sem, rr_sem, os_sem, or_sem, oloc_sem,
           xs_sem, xr_sem, ts_sem, tr_sem):
    me = lax.axis_index("ta")
    mx = lax.axis_index("xyz")
    worker = jnp.logical_and(me >= lo, me < hi)
    mine = me - lo
    workers = hi - lo
    share = nc // parts
    slots = raw.shape[0]
    cells = 8
    left, right = lax.rem(mx + nx - 1, nx), lax.rem(mx + 1, nx)
    sub = lax.broadcasted_iota(jnp.int32, (8, 128), 0)
    zc = lax.broadcasted_iota(jnp.int32, (8, 128), 1) % NZ

    for slot in range(slots):
        pltpu.make_async_copy(link_ref.at[slot], raw.at[slot], raw_sem.at[slot]).start()

    def own_copy(part):
        return pltpu.make_async_copy(sink_ref.at[pl.ds(mine * nc + part * share, share)],
                                     lam.at[me, pl.ds(part * share, share)], loc_sem.at[part])

    @pl.when(worker)
    def _():
        for part in range(parts):
            own_copy(part).start()

    barrier = pltpu.get_barrier_semaphore()
    for d in range(1, n):
        pl.semaphore_signal(barrier, inc=1, device_id={"ta": lax.rem(me + d, n)}, device_id_type=MESH)
    for d in range(1, nx):
        pl.semaphore_signal(barrier, inc=1, device_id={"xyz": lax.rem(mx + d, nx)}, device_id_type=MESH)
    pl.semaphore_wait(barrier, n + nx - 2)

    def field_copy(j, source, part):
        return remote(sink_ref.at[pl.ds(j * nc + part * share, share)],
                      lam.at[source, pl.ds(part * share, share)],
                      fs_sem.at[j, part], fr_sem.at[source, part], "ta", lo + j)

    def link_copy(s, j, source):
        return remote(lk.at[s, source], lk.at[s, source], ls_sem.at[s, j], lr_sem.at[s, source], "ta", lo + j)

    def peer_order(i):
        return jnp.where(me < n // 2, workers - 1 - i, i)

    def to_workers(act):
        for i in range(workers):
            j = peer_order(i)

            @pl.when(me != lo + j)
            def _():
                act(j)

    for part in range(parts):
        to_workers(lambda j: field_copy(j, me, part).start())

    for slot in range(slots):
        pltpu.make_async_copy(link_ref.at[slot], raw.at[slot], raw_sem.at[slot]).wait()

    for s in range(SECTIONS):
        slot = order_ref[STEPS - 1 - s // 3, 2 - s % 3]
        for g in range(4):
            lk[s, me, g * 18:(g + 1) * 18] = raw[slot, g * 18:(g + 1) * 18]
        to_workers(lambda j: link_copy(s, j, me).start())

    def fill_table():
        nx_total = cells * nx
        lane = lax.broadcasted_iota(jnp.int32, (8, 128), 1)
        table[0, 0:8] = jnp.zeros((8, 128), jnp.float32)
        table[0, 0:3, 0:nmom] = momenta_ref[...].astype(jnp.float32)
        base = table[0, 0:8]
        both = jnp.where(lane < 64, base, pltpu.roll(base, 64, 1))
        quarter = jnp.where(lane < 64, 0.0, 0.25)
        shape = (NY * NZ, 128)
        site = lax.broadcasted_iota(jnp.int32, shape, 0)
        yd = (site // NZ - source_ref[1]).astype(jnp.float32)
        zd = (site % NZ - source_ref[2]).astype(jnp.float32)

        def part_of(p, d, size):
            f = (p * d) * (1.0 / size)
            return f - jnp.floor(f)

        base_frac = (part_of(jnp.broadcast_to(both[1:2], shape), yd, NY)
                     + part_of(jnp.broadcast_to(both[2:3], shape), zd, NZ)
                     + jnp.broadcast_to(quarter[0:1], shape))
        px = jnp.broadcast_to(both[0:1], shape)

        for x in range(cells):
            xd = (mx * cells + x - source_ref[0]).astype(jnp.float32)
            frac = base_frac + part_of(px, jnp.full(shape, xd), nx_total)
            frac = frac - jnp.floor(frac + 0.5)
            u = (2.0 * math.pi) * (0.25 - jnp.abs(frac))
            w = u * u
            p = -1.0 / 39916800.0 + w * (1.0 / 6227020800.0)
            for coef in (1.0 / 362880.0, -1.0 / 5040.0, 1.0 / 120.0, -1.0 / 6.0, 1.0):
                p = coef + w * p
            table[x] = u * p

    def halo_copy(s, side, part):
        peer = (left, right)[side]
        return remote(hs.at[s % 2, side, part], hr.at[s % 2, side, part], hss_sem.at[s, side, part],
                      hsr_sem.at[s, side, part], "xyz", peer)

    def put_halo(s, part, t, w, value):
        base = (t * share + w) * 6
        for c in range(6):
            hs[s % 2, 0, part, pl.ds(base + c, 1)] = value[c, 0:1]
            hs[s % 2, 1, part, pl.ds(base + c, 1)] = value[c, 7:8]

    def start_halos(s, part):
        for side in range(2):
            halo_copy(s, side, part).start()

    @pl.when(worker)
    def _():
        fill_table()

        def at_part(part, carry):
            own_copy(part).wait()
            for d in range(1, n):
                field_copy(0, lax.rem(me + d, n), part).wait_recv()

            def first_halo(i, inner):
                t, w = i // share, i % share
                put_halo(0, part, t, w, lam[t, part * share + w])
                return inner

            lax.fori_loop(0, n * share, first_halo, 0)
            start_halos(0, part)
            return carry

        lax.fori_loop(0, parts, at_part, 0)

    def row_copy(s):
        return remote(rs.at[s], rr.at[s], rs_sem.at[s], rr_sem.at[s], "xyz", right)

    def prepare(s):
        def send_rows(t, carry):
            rs[s, t, 0:18] = lk[s, t, 18:36, 7, :]
            return carry

        lax.fori_loop(0, n, send_rows, 0)
        row_copy(s).start()

        def forward(t, carry):
            for d in range(4):
                block = lk[s, t, d * 18:(d + 1) * 18].reshape(9, 2, 8, 128)
                re, im = block[:, 0], block[:, 1]
                cur[t, d] = jnp.stack([re, re + im, im - re], axis=1).reshape(27, 8, 128)
            return carry

        def put_back(t, d, block):
            block = block.reshape(3, 3, 2, 8, 128)
            for a in range(3):
                re, im = block[:, a, 0], block[:, a, 1]
                cur[t, 3 + d, a * 9:(a + 1) * 9] = jnp.stack([re, re - im, -(re + im)], axis=1).reshape(9, 8, 128)

        def backward(t, carry):
            put_back(t, 2, roll3(lk[s, t, 36:54], NZ, 2))
            uz = lk[s, t, 54:72]
            put_back(t, 3, jnp.where((zc == 0)[None], roll3(uz, 1 - NZ, 2), roll3(uz, 1, 2)))
            return carry

        def backward_x(t, carry):
            ux = roll3(lk[s, t, 18:36], 1, 1)
            rows = jnp.broadcast_to(rr[s, t, 0:18][:, None, :], (18, 8, 128))
            put_back(t, 1, jnp.where((sub == 0)[None], rows, ux))
            return carry

        lax.fori_loop(0, n, forward, 0)
        lax.fori_loop(0, n, backward, 0)
        row_copy(s).wait_recv()
        lax.fori_loop(0, n, backward_x, 0)

    def lap(s, part, source, epilogue, after_time):
        par = s % 2

        def at_time(i, carry):
            t = jnp.where(me < n // 2, n - 1 - i, i)
            prev, following = lax.rem(t + n - 1, n), lax.rem(t + 1, n)

            def links(time, d):
                return cur[time, d].reshape(3, 3, 3, 8, 128)

            def at_spinor(w, inner):
                q = part * share + w
                row = (t * share + w) * 6
                v = source[t, q]
                acc = (None, None, None)
                acc = hop(acc, links(t, 0), source[following, q], False)
                acc = hop(acc, links(prev, 0), source[prev, q], True)
                high = jnp.stack([jnp.broadcast_to(hr[par, 0, part, pl.ds(row + c, 1)], (8, 128)) for c in range(6)])
                low = jnp.stack([jnp.broadcast_to(hr[par, 1, part, pl.ds(row + c, 1)], (8, 128)) for c in range(6)])
                acc = hop(acc, links(t, 1), jnp.where((sub == 7)[None], high, roll3(v, -1, 1)), False)
                acc = hop(acc, links(t, 4), jnp.where((sub == 0)[None], low, roll3(v, 1, 1)), False)
                acc = hop(acc, links(t, 2), roll3(v, -NZ, 2), False)
                acc = hop(acc, links(t, 5), roll3(v, NZ, 2), False)
                vf = jnp.where((zc == NZ - 1)[None], roll3(v, NZ - 1, 2), roll3(v, -1, 2))
                acc = hop(acc, links(t, 3), vf, False)
                vb = jnp.where((zc == 0)[None], roll3(v, 1 - NZ, 2), roll3(v, 1, 2))
                acc = hop(acc, links(t, 6), vb, False)
                total = jnp.stack([acc[0] - acc[1], acc[0] + acc[2]], axis=1).reshape(6, 8, 128)
                nxt = epilogue(t, q, total - 8.0 * v, v)
                if nxt is not None:
                    put_halo(s + 1, part, t, w, nxt)
                return inner

            lax.fori_loop(0, share, at_spinor, 0)
            after_time(t, part)
            return carry

        lax.fori_loop(0, n, at_time, 0)

    def ep_later(t, q, value, v):
        value = (0.75 * flow_step) * value
        later[t, q] = value
        return value

    def ep_middle(t, q, value, v):
        middle = lam[t, q] + (8.0 * flow_step / 9.0) * value
        lam[t, q] = middle + v
        value = (0.25 * flow_step) * middle - (2.0 * flow_step / 9.0) * v
        mixed[t, q] = value
        return value

    def ep_last(t, q, value, v):
        value = lam[t, q] + value
        lam[t, q] = value
        square = value * value
        square = (square[0] + square[1]) + (square[2] + square[3]) + (square[4] + square[5])
        sign = jnp.where(lax.rem(q, 4) < 2, 1.0, -1.0)
        dens[t] = dens[t] + sign * square
        return value

    def out_copy(t, part, j):
        return remote(lam.at[t, pl.ds(part * share, share)],
                      out_ref.at[pl.ds(j * nc + part * share, share)],
                      os_sem.at[t, part], or_sem.at[j, part], "ta", t)

    def own_out(part):
        return pltpu.make_async_copy(lam.at[me, pl.ds(part * share, share)],
                                     out_ref.at[pl.ds(mine * nc + part * share, share)], oloc_sem.at[part])

    def nothing(t, part):
        return None

    def step_body(i, carry):
        for k, (source, epilogue) in enumerate(((lam, ep_later), (later, ep_middle), (mixed, ep_last))):
            s = i * 3 + k

            def give(t, part):
                @pl.when(jnp.logical_and(s + 1 == SECTIONS, t != me))
                def _():
                    out_copy(t, part, mine).start()

            for d in range(1, n):
                link_copy(s, 0, lax.rem(me + d, n)).wait_recv()
            prepare(s)
            if k == 2:
                dens[...] = jnp.zeros(dens.shape, jnp.float32)

            def at_part(part, inner):
                for side in range(2):
                    halo_copy(s, side, part).wait()
                lap(s, part, source, epilogue, give if k == 2 else nothing)

                @pl.when(s + 1 < SECTIONS)
                def _():
                    start_halos(s + 1, part)

                @pl.when(s + 1 == SECTIONS)
                def _():
                    own_out(part).start()
                return inner

            lax.fori_loop(0, parts, at_part, 0)
        return carry

    def x_copy(d):
        return remote(pjs, pjr.at[mx], xs_sem.at[d - 1], xr_sem.at[mx], "xyz", lax.rem(mx + d, nx))

    def x_arrival(j):
        return remote(pjs, pjr.at[j], xs_sem.at[0], xr_sem.at[j], "xyz", j)

    def t_copy(t):
        return remote(pjt.at[t], pjf.at[mine], ts_sem.at[t], tr_sem.at[mine], "ta", t)

    @pl.when(worker)
    def _():
        lax.fori_loop(0, STEPS, step_body, 0)
        rows = dens[...].reshape(n * 8, 128)
        cell = lax.broadcasted_iota(jnp.int32, (n * 8, 128), 0) % 8
        acc = jnp.zeros((n * 8, 128), jnp.float32)
        for x in range(cells):
            product = jnp.dot(rows, table[x], precision=lax.Precision.HIGHEST, preferred_element_type=jnp.float32)
            acc = acc + jnp.where(cell == x, product, 0.0)
        pjs[...] = jnp.broadcast_to(jnp.sum(acc.reshape(n, 8, 128), axis=1, keepdims=True), (n, 8, 128))
        pjr[mx] = pjs[...]
        for d in range(1, nx):
            x_copy(d).start()
        for d in range(1, nx):
            x_arrival(lax.rem(mx + d, nx)).wait_recv()
        total = pjr[0]
        for j in range(1, nx):
            total = total + pjr[j]
        pjt[...] = total
        pjf[mine] = pjt[me]
        for d in range(1, n):
            t_copy(lax.rem(me + d, n)).start()

    for j in range(workers):
        @pl.when(me != lo + j)
        def _():
            remote(pjt.at[0], pjf.at[j], ts_sem.at[0], tr_sem.at[j], "ta", lo + j).wait_recv()
    final = pjf[0]
    for j in range(1, workers):
        final = final + pjf[j]
    final = final * (1.0 / math.sqrt(576.0 * cells * nx * NY * NZ))
    proj_ref[0] = final[0:1, 0:nmom]
    proj_ref[1] = pltpu.roll(final, 64, 1)[0:1, 0:nmom]

    def drain(act):
        to_workers(act)

    def drain_parts(part, carry):
        to_workers(lambda j: field_copy(j, me, part).wait_send())
        return carry

    def drain_links(s, carry):
        to_workers(lambda j: link_copy(s, j, me).wait_send())
        return carry

    lax.fori_loop(0, parts, drain_parts, 0)
    lax.fori_loop(0, SECTIONS, drain_links, 0)

    @pl.when(worker)
    def _():
        def drain_rows(s, carry):
            row_copy(s).wait_send()
            return carry

        lax.fori_loop(0, SECTIONS, drain_rows, 0)
        for d in range(1, nx):
            x_copy(d).wait_send()
        for d in range(1, n):
            t_copy(lax.rem(me + d, n)).wait_send()

        def drain_out(part, carry):
            for d in range(1, n):
                out_copy(lax.rem(me + d, n), part, mine).wait_send()
            own_out(part).wait()
            return carry

        lax.fori_loop(0, parts, drain_out, 0)

    def arrivals(part, carry):
        for j in range(workers):
            @pl.when(me != lo + j)
            def _():
                out_copy(lo + j, part, j).wait_recv()
        return carry

    lax.fori_loop(0, parts, arrivals, 0)


def body(n, nx, sink, links, section_index, momenta, source):
    space_cells = sink.shape[5]
    spinors = sink.shape[0] * sink.shape[1]
    slots = links.shape[0]
    nmom = momenta.shape[0]
    lo = n // 4 if spinors % (n - 2 * (n // 4)) == 0 else 0
    hi = n - lo
    nc = spinors // (hi - lo)
    parts = next(p for p in (4, 3, 2, 1) if nc % p == 0)
    share = nc // parts
    workers = hi - lo
    tile = (space_cells, NY * NZ)
    f32 = jnp.float32
    field = pltpu.VMEM((n, nc, 6) + tile, f32)
    halo = pltpu.VMEM((2, 2, parts, n * share * 6, NY * NZ), f32)
    dma = pltpu.SemaphoreType.DMA
    anywhere = pl.BlockSpec(memory_space=pl.ANY)
    vmem = pl.BlockSpec(memory_space=pltpu.VMEM)
    smem = pl.BlockSpec(memory_space=pltpu.SMEM)
    out, proj = pl.pallas_call(
        functools.partial(kernel, n, nx, nc, lo, hi, parts, nmom),
        out_shape=(
            jax.ShapeDtypeStruct((spinors, 6) + tile, f32),
            jax.ShapeDtypeStruct((2, 1, nmom), f32),
        ),
        in_specs=[smem, smem, vmem, anywhere, anywhere],
        out_specs=(anywhere, vmem),
        scratch_shapes=[
            pltpu.VMEM((slots, 72) + tile, f32),
            pltpu.VMEM((SECTIONS, n, 72) + tile, f32),
            pltpu.VMEM((n, 7, 27) + tile, f32),
            field, field, field,
            halo, halo,
            pltpu.VMEM((SECTIONS, n, 24, NY * NZ), f32),
            pltpu.VMEM((SECTIONS, n, 24, NY * NZ), f32),
            pltpu.VMEM((space_cells, NY * NZ, 128), f32),
            pltpu.VMEM((n,) + tile, f32),
            pltpu.VMEM((n, 8, 128), f32),
            pltpu.VMEM((nx, n, 8, 128), f32),
            pltpu.VMEM((n, 8, 128), f32),
            pltpu.VMEM((workers, 8, 128), f32),
            dma((slots,)), dma((parts,)),
            dma((workers, parts)), dma((n, parts)),
            dma((SECTIONS, workers)), dma((SECTIONS, n)),
            dma((SECTIONS, 2, parts)), dma((SECTIONS, 2, parts)),
            dma((SECTIONS,)), dma((SECTIONS,)),
            dma((n, parts)), dma((workers, parts)), dma((parts,)),
            dma((nx - 1,)), dma((nx,)),
            dma((n,)), dma((workers,)),
        ],
        compiler_params=pltpu.CompilerParams(
            collective_id=0, has_side_effects=True, vmem_limit_bytes=63 * 1024 * 1024
        ),
    )(section_index, source, momenta.T, sink.reshape((spinors, 6) + tile), links.reshape((slots, 72) + tile))
    return (out.reshape(sink.shape), jnp.transpose(proj, (0, 2, 1)))


def solution(mesh):
    in_specs = (
        P("cfg", None, None, None, "ta", "xyz", None),
        P("cfg", None, None, None, None, "ta", "xyz", None),
        P(),
        P(),
        P(),
    )
    out_specs = (P("cfg", None, None, None, "ta", "xyz", None), P("cfg", None, "ta"))
    step = functools.partial(body, mesh.shape["ta"], mesh.shape["xyz"])
    return jax.shard_map(step, mesh=mesh, in_specs=in_specs, out_specs=out_specs, check_vma=False)
```

time: 178 us -> 155 us (0.87)
  other arithmetic: 9.04 us -> 0 us
  Pallas kernels: 159 us -> 151 us
  local copies, waits for them, and re-layouts: 8.47 us -> 2.95 us
    pallas_call x1, Pallas kernels: 159 us -> 151 us  [body(): pl.pallas_call(functools.partial(kernel, n, nx, nc, lo, hi, parts, nmom),...]
    select_n x5 -> x0, other arithmetic: 3.79 us -> none  [the longest x2 1.78 us: body(): jnp.take(links, order, axis=0).reshape(SECTIONS, 72, space_cells, NY * NZ)]
    concatenate x2 -> x0, other arithmetic: 3.56 us -> none  [the longest x1 2.83 us: body(): blocks = jnp.concatenate([chosen, rows], axis=1)]
    gather x1 -> x0, local copies, waits for them, and re-layouts: 1.89 us -> none  [body(): jnp.take(links, order, axis=0).reshape(SECTIONS, 72, space_cells, NY * NZ)]
    unnamed x10 -> x4, local copies, waits for them, and re-layouts: 4.17 us -> 2.95 us
  transfers between devices with their start and end apart: 1 -> 0, of which waited for: 0 -> 0; matrix products, arithmetic and copies ran while one was open for 2% -> 0% of each run, Pallas kernels for 0% -> 0%
where the time goes in v1:
time: 155 us; the launch traced here: 154 us
  Pallas kernels  151 us (97%)
  local copies, waits for them, and re-layouts  2.95 us (2%)
    pallas_call x1, Pallas kernels, body(): pl.pallas_call(functools.partial(kernel, n, nx, nc, lo, hi, parts, nmom),...  151 us

profile of v1, /device:TPU:0, one launch (start us, length us, event | category | flops | bytes accessed | tf_op | source)
XLA Modules:
  0.0 154.4 jit_solution(17617791415454441361)
XLA Ops:
  0.6 150.8 %shard_map.68 = (f32[48,6,8,128]{3,2,1,0:T(8,128)}, f32[2,1,33]{2,1,0:T(1,128)}) custom-call(s32[2,3]{1,0:T(2,128)} %order_ref.1, s32[3]{0:T(128)} %source_ref.1, s32[3,33]{1,0:T(4,128)} %bitcast.12, f32[48,6,8,128]{3,2,1,0:T(8,128)} %bitcast.11, f32[8,72,8,128]{3,2,1,0:T(8,128)} %bitcast.9), custom_call_target="tpu_custom_call" | custom-call | tf_op jit(solution)/shard_map/pallas_call | solution.py:439
  151.5 0.0 copy-start
  151.5 2.4 %copy.11 = f32[12,4,3,2,1,8,128]{6,5,4,3,2,1,0:T(8,128)} copy(f32[12,4,3,2,1,8,128]{6,5,4,3,2,1,0:T(8,128)} %bitcast.10) | data formatting | bytes 2359296
  153.9 0.0 copy-done
  153.9 0.6 copy.12
Async XLA Ops:
  151.5 2.4 %copy-start = (f32[2,1,33]{2,1,0:T(1,128)S(1)}, f32[2,1,33]{2,1,0:T(1,128)}, u32[]{:S(2)}) copy-start(f32[2,1,33]{2,1,0:T(1,128)} %get-tuple-element.5) | copy-start | bytes 796
